TPU v7x, 32 devices: a whole 2x2x4 slice. The times are simulated.
32 devices in a mesh: section: 1, srv: 16 (over z, x, core), tp: 2 (over y).
Axes of the slice: x: 2, y: 2, z: 4, core: 2. Of those that a mesh axis runs over, the one named last changes fastest.
Arguments:
- queries: bfloat16 [2048, 4096], P(('section', 'srv'), 'tp'), may hold values from -40 to 40
- keys: bfloat16 [2048, 512], P(('section', 'srv'), 'tp'), may hold values from -40 to 40
- values: bfloat16 [2048, 512], P(('section', 'srv'), 'tp'), may hold values from -6 to 6
- residual: bfloat16 [2048, 4096], P(('section', 'srv'), 'tp'), may hold values from -6 to 6
- out_weight: bfloat16 [4096, 4096], P('tp', ('section', 'srv')), may hold values from -0.1875 to 0.1875
- norm_gain: float32 [4096], P('tp'), may hold values from 0.25 to 1.75
- level_shift: float32 [8, 4096], P(None, 'tp'), may hold values from -3 to 3
- doc_lengths: int32 [1, 4], P('section'), may hold values from 1 to 64, 128 in all within a row
- noise_level: int32 [1, 4], P('section'), may hold values from 0 to 7
Outputs:
- normed: bfloat16 [2048, 4096], P(('section', 'srv'), 'tp')
Inputs may be any that keep to these rules, and one draw needn't show every extreme that they name: `doc_lengths`: each micro-batch's lengths sum to 128.
All inputs are finite; a program needn't handle non-finite values.
Results may differ from a plain program's by a relative error of at most 0.013.
Values may be sent and summed in bfloat16 or wider, within the bound.
No kernel may reach another device: no remote copies, remote signals or barrier semaphores. Data moves between devices by JAX's collectives and lax.ppermute only.
A program may use at most 64 MiB of HBM per device.

v0:
```python
import jax
import jax.numpy as jnp
from jax import lax
from jax.sharding import PartitionSpec as P

D = 4096
HEAD_SIZE = 128
BLK = 16


def shifted(block, axis, distance):
    devices = range(lax.axis_size(axis))
    route = [(i - distance, i) for i in devices if i - distance in devices]
    return lax.ppermute(block, axis, route)


def bounds(positions, starts, ends):
    member = (positions[:, None] >= starts[None, :]) & (positions[:, None] < ends[None, :])
    first = jnp.sum(jnp.where(member, starts[None, :], 0), axis=1)
    limit = (positions // BLK + 1) * BLK
    return (member, first, limit)


def make_absorb(query_block, first, limit, kv_heads, query_groups):
    rows = query_block.shape[0]
    scale = HEAD_SIZE ** (-0.5)
    grouped = (
        query_block.reshape(rows, kv_heads, query_groups, HEAD_SIZE)
        .transpose(1, 2, 0, 3)
        .reshape(kv_heads, query_groups * rows, HEAD_SIZE)
    )
    row_first = jnp.tile(first, query_groups)
    row_limit = jnp.tile(limit, query_groups)
    empty = (
        jnp.full((kv_heads, query_groups * rows), -1e30, jnp.float32),
        jnp.zeros((kv_heads, query_groups * rows), jnp.float32),
        jnp.zeros((kv_heads, query_groups * rows, HEAD_SIZE), jnp.float32),
    )

    def absorb(carry, pieces, start):
        key_piece, value_piece = pieces
        count = key_piece.shape[0]
        key_pos = start + jnp.arange(count, dtype=jnp.int32)
        mask = (key_pos[None, :] >= row_first[:, None]) & (key_pos[None, :] < row_limit[:, None])

        def update(state):
            best, total, summed = state
            key_heads = key_piece.reshape(count, kv_heads, HEAD_SIZE)
            value_heads = value_piece.reshape(count, kv_heads, HEAD_SIZE)
            scores = (
                jnp.einsum("kxd,jkd->kxj", grouped, key_heads, preferred_element_type=jnp.float32)
                * scale
            )
            scores = jnp.where(mask[None], scores, -1e30)
            new_best = jnp.maximum(best, jnp.max(scores, axis=-1))
            weights = jnp.where(mask[None], jnp.exp(scores - new_best[..., None]), 0.0)
            factor = jnp.exp(best - new_best)
            total = total * factor + jnp.sum(weights, axis=-1)
            update_sum = jnp.einsum(
                "kxj,jkd->kxd",
                weights.astype(jnp.bfloat16),
                value_heads,
                preferred_element_type=jnp.float32,
            )
            return (new_best, total, summed * factor[..., None] + update_sum)

        return lax.cond(jnp.any(mask), update, lambda state: state, carry)

    return (absorb, empty)


def finish(carry, rows, kv_heads, query_groups):
    best, total, summed = carry
    attended = (
        (summed / total[..., None])
        .reshape(kv_heads, query_groups, rows, HEAD_SIZE)
        .transpose(2, 0, 1, 3)
    )
    return attended.reshape(rows, kv_heads * query_groups * HEAD_SIZE).astype(jnp.bfloat16)


def on_device(
    queries, keys, values, residual, out_weight, norm_gain, level_shift, doc_lengths, noise_level
):
    rows = queries.shape[0]
    kv_heads = keys.shape[1] // HEAD_SIZE
    query_groups = queries.shape[1] // keys.shape[1]
    here = lax.axis_index("srv")
    devices = lax.axis_size("srv")
    lengths = doc_lengths[0] * BLK
    ends = jnp.cumsum(lengths)
    starts = ends - lengths
    positions = here * rows + jnp.arange(rows, dtype=jnp.int32)
    member, first, limit = bounds(positions, starts, ends)
    absorb, empty = make_absorb(queries, first, limit, kv_heads, query_groups)
    span = min(devices, devices // 2 + 1)
    carry = absorb(empty, (keys, values), here * rows)

    def turn_step(turn, state):
        carry_now, held = state
        held = shifted(held, "srv", 1)
        carry_now = absorb(carry_now, (held[0], held[1]), (here - turn) * rows)
        return (carry_now, held)

    carry, held = lax.fori_loop(1, span, turn_step, (carry, jnp.stack([keys, values], axis=0)))
    attended = finish(carry, rows, kv_heads, query_groups)
    partial_sum = jnp.dot(
        attended,
        lax.all_gather(out_weight, ("section", "srv"), axis=1, tiled=True),
        preferred_element_type=jnp.float32,
    )
    width = residual.shape[1]
    offset = lax.axis_index("tp") * width
    own_part = lax.dynamic_slice_in_dim(partial_sum, offset, width, 1) + residual.astype(
        jnp.float32
    )
    placed = lax.dynamic_update_slice_in_dim(partial_sum, own_part, offset, 1)
    whole = lax.psum(placed.astype(jnp.bfloat16), "tp").astype(jnp.float32)
    hidden = lax.dynamic_slice_in_dim(whole, offset, width, 1)
    squares = jnp.sum(whole * whole, axis=1)
    inverse = lax.rsqrt(squares / D + 1e-06)
    level = jnp.sum(jnp.where(member, noise_level[0][None, :], 0), axis=1)
    onehot = (level[:, None] == jnp.arange(level_shift.shape[0], dtype=jnp.int32)[None, :]).astype(
        jnp.float32
    )
    shift = jnp.dot(onehot, level_shift, precision=lax.Precision.HIGHEST)
    normed = hidden * inverse[:, None] * norm_gain[None, :] * (1.0 + shift)
    return normed.astype(jnp.bfloat16)


def solution(mesh):
    placed = (
        P(("section", "srv"), "tp"),
        P(("section", "srv"), "tp"),
        P(("section", "srv"), "tp"),
        P(("section", "srv"), "tp"),
        P("tp", ("section", "srv")),
        P("tp"),
        P(None, "tp"),
        P("section", None),
        P("section", None),
    )
    return jax.shard_map(
        on_device,
        mesh=mesh,
        in_specs=placed,
        out_specs=P(("section", "srv"), "tp"),
        check_vma=False,
    )
```

profile of v0, /device:TPU:0, one launch (start us, length us, event | category | flops | bytes accessed | tf_op | source)
XLA Modules:
  0.0 211.0 jit_solution(15229370713892735644)
XLA Ops:
  8.2 1.1 copy.50
  11.4 3.9 %conditional.2 = (f32[2,1024]{1,0:T(2,128)}, f32[2,1024]{1,0:T(2,128)S(1)}, f32[2,1024,128]{2,1,0:T(8,128)S(1)}) conditional(s32[]{:T(128)} %convert_element_type.41, () %tuple.34, (pred[1024,128]{0,1:T(8,128)(4,1)S(1)}, bf16[128,256]{1,0:T(8,128)(2,1)S(1)}, bf16[2,1024,128]{2,1,0:T(8,128)(2,1)S(1)}, bf16[128,256]{1,0:T(8,128)(2,1)S(1)}) %tuple.84), branch_computations={%region_3.4_spmd, %region_4.7_spmd} | conditional | flops 136847360 | bytes 5333016 | solution.py:67
  12.4 1.3 convolution_add_fusion
  13.7 0.9 fusion.6
  15.3 74.7 %while.20 = (s32[]{:T(128)}, f32[2,1024]{1,0:T(2,128)}, f32[2,1024]{1,0:T(2,128)S(1)}, f32[2,1024,128]{2,1,0:T(8,128)S(1)}, bf16[2,128,256]{1,2,0:T(8,128)(2,1)S...) while((s32[]{:T(128)}, f32[2,1024]{1,0:T(2,128)}, ...), condition=%wide.region_13.14_spmd.clone, body=%wide.region_7.13_spmd.clone.sunk | while | flops 137629824 | bytes 7620895 | solution.py:105
  15.4 2.4 %collective-permute-start = (bf16[2,128,256]{1,2,0:T(8,128)(2,1)S(1)}, bf16[2,128,256]{1,2,0:T(8,128)(2,1)S(1)}, u32[]{:S(2)}, u32[]{:S(2)}) collective-permute-start(bf16[2,128,256]{1,2,0:T(8,128)(2,1)S(1)} %get-tuple-element.376), channel_id=1, source_target_pairs={{0,2},{2,4},{4,6},{6,8},{8,10},{10,12},{12,14},{14,16},{16,18},{18... | collective-permute-start | bytes 393224 | tf_op jit(solution)/shard_map/while/body/eval_jaxpr/ppermute | solution.py:14
  17.8 0.9 compare_and_fusion.4
  19.4 10.3 %collective-permute-start = (bf16[2,128,256]{1,2,0:T(8,128)(2,1)S(1)}, bf16[2,128,256]{1,2,0:T(8,128)(2,1)S(1)}, u32[]{:S(2)}, u32[]{:S(2)}) collective-permute-start(bf16[2,128,256]{1,2,0:T(8,128)(2,1)S(1)} %get-tuple-element.376), channel_id=1, source_target_pairs={{0,2},{2,4},{4,6},{6,8},{8,10},{10,12},{12,14},{14,16},{16,18},{18... | collective-permute-start | bytes 393224 | tf_op jit(solution)/shard_map/while/body/eval_jaxpr/ppermute | solution.py:14
  29.7 0.9 compare_and_fusion.4
  31.2 5.6 %collective-permute-start = (bf16[2,128,256]{1,2,0:T(8,128)(2,1)S(1)}, bf16[2,128,256]{1,2,0:T(8,128)(2,1)S(1)}, u32[]{:S(2)}, u32[]{:S(2)}) collective-permute-start(bf16[2,128,256]{1,2,0:T(8,128)(2,1)S(1)} %get-tuple-element.376), channel_id=1, source_target_pairs={{0,2},{2,4},{4,6},{6,8},{8,10},{10,12},{12,14},{14,16},{16,18},{18... | collective-permute-start | bytes 393224 | tf_op jit(solution)/shard_map/while/body/eval_jaxpr/ppermute | solution.py:14
  36.9 0.9 compare_and_fusion.4
  38.4 8.3 %collective-permute-start = (bf16[2,128,256]{1,2,0:T(8,128)(2,1)S(1)}, bf16[2,128,256]{1,2,0:T(8,128)(2,1)S(1)}, u32[]{:S(2)}, u32[]{:S(2)}) collective-permute-start(bf16[2,128,256]{1,2,0:T(8,128)(2,1)S(1)} %get-tuple-element.376), channel_id=1, source_target_pairs={{0,2},{2,4},{4,6},{6,8},{8,10},{10,12},{12,14},{14,16},{16,18},{18... | collective-permute-start | bytes 393224 | tf_op jit(solution)/shard_map/while/body/eval_jaxpr/ppermute | solution.py:14
  46.7 0.9 compare_and_fusion.4
  48.3 4.7 %collective-permute-start = (bf16[2,128,256]{1,2,0:T(8,128)(2,1)S(1)}, bf16[2,128,256]{1,2,0:T(8,128)(2,1)S(1)}, u32[]{:S(2)}, u32[]{:S(2)}) collective-permute-start(bf16[2,128,256]{1,2,0:T(8,128)(2,1)S(1)} %get-tuple-element.376), channel_id=1, source_target_pairs={{0,2},{2,4},{4,6},{6,8},{8,10},{10,12},{12,14},{14,16},{16,18},{18... | collective-permute-start | bytes 393224 | tf_op jit(solution)/shard_map/while/body/eval_jaxpr/ppermute | solution.py:14
  54.6 8.4 %collective-permute-start = (bf16[2,128,256]{1,2,0:T(8,128)(2,1)S(1)}, bf16[2,128,256]{1,2,0:T(8,128)(2,1)S(1)}, u32[]{:S(2)}, u32[]{:S(2)}) collective-permute-start(bf16[2,128,256]{1,2,0:T(8,128)(2,1)S(1)} %get-tuple-element.376), channel_id=1, source_target_pairs={{0,2},{2,4},{4,6},{6,8},{8,10},{10,12},{12,14},{14,16},{16,18},{18... | collective-permute-start | bytes 393224 | tf_op jit(solution)/shard_map/while/body/eval_jaxpr/ppermute | solution.py:14
  64.6 10.1 %collective-permute-start = (bf16[2,128,256]{1,2,0:T(8,128)(2,1)S(1)}, bf16[2,128,256]{1,2,0:T(8,128)(2,1)S(1)}, u32[]{:S(2)}, u32[]{:S(2)}) collective-permute-start(bf16[2,128,256]{1,2,0:T(8,128)(2,1)S(1)} %get-tuple-element.376), channel_id=1, source_target_pairs={{0,2},{2,4},{4,6},{6,8},{8,10},{10,12},{12,14},{14,16},{16,18},{18... | collective-permute-start | bytes 393224 | tf_op jit(solution)/shard_map/while/body/eval_jaxpr/ppermute | solution.py:14
  76.3 12.2 %collective-permute-start = (bf16[2,128,256]{1,2,0:T(8,128)(2,1)S(1)}, bf16[2,128,256]{1,2,0:T(8,128)(2,1)S(1)}, u32[]{:S(2)}, u32[]{:S(2)}) collective-permute-start(bf16[2,128,256]{1,2,0:T(8,128)(2,1)S(1)} %get-tuple-element.376), channel_id=1, source_target_pairs={{0,2},{2,4},{4,6},{6,8},{8,10},{10,12},{12,14},{14,16},{16,18},{18... | collective-permute-start | bytes 393224 | tf_op jit(solution)/shard_map/while/body/eval_jaxpr/ppermute | solution.py:14
  90.7 58.3 %all-gather.2.cloned.1.call-done = bf16[2048,4096]{1,0:T(8,128)(2,1)} async-done(((bf16[2048,256]{1,0:T(8,128)(2,1)}), bf16[2048,4096]{1,0:T(8,128)(2,1)}) %all-gather.2.cloned.1.call-update) | async-done | bytes 16777232 | tf_op jit(solution)/shard_map/all_gather | solution.py:109
  149.1 8.2 %fusion.34 = f32[128,4096]{1,0:T(8,128)S(1)} fusion(bf16[128,2048]{0,1:T(8,128)(2,1)S(1)} %bitcast.61, bf16[2048,4096]{1,0:T(8,128)(2,1)} %all-gather.2.cloned.1.call-done), kind=kOutput, calls=%fused_computation.65 | convolution fusion | flops 2147483648 | bytes 19398656 | tf_op jit(solution)/shard_map/dot_general | solution.py:107
  157.4 1.2 convert_element_type.47
  158.6 41.1 %all-reduce.2.cloned.1.call-done = bf16[128,4096]{1,0:T(8,128)(2,1)} async-done(((bf16[128,4096]{1,0:T(8,128)(2,1)}), bf16[128,4096]{1,0:T(8,128)(2,1)}) %all-reduce.2.cloned.1.call-update) | async-done | bytes 1048592 | tf_op jit(solution)/shard_map/psum | solution.py:118
  199.7 1.5 multiply_reduce_fusion
  201.3 1.4 convert_element_type.48
  202.7 1.4 fusion.27
  (81 shorter events, 9.2 us)
Async XLA Ops:
  6.5 196.2 %copy-start = (f32[8,2048]{1,0:T(8,128)S(1)}, f32[8,2048]{1,0:T(8,128)}, u32[]{:S(2)}) copy-start(f32[8,2048]{1,0:T(8,128)} %param.21) | copy-start | bytes 196612
  6.5 3.0 %copy-start.6 = (s32[1,4]{1,0:T(1,128)S(1)}, s32[1,4]{1,0:T(1,128)}, u32[]{:S(2)}) copy-start(s32[1,4]{1,0:T(1,128)} %param.22) | copy-start | bytes 52
  6.5 3.0 %copy-start.5 = (s32[1,4]{1,0:T(1,128)S(1)}, s32[1,4]{1,0:T(1,128)}, u32[]{:S(2)}) copy-start(s32[1,4]{1,0:T(1,128)} %param.23) | copy-start | bytes 52
  6.5 4.6 %copy-start.2 = (bf16[128,256]{1,0:T(8,128)(2,1)S(1)}, bf16[128,256]{1,0:T(8,128)(2,1)}, u32[]{:S(2)}) copy-start(bf16[128,256]{1,0:T(8,128)(2,1)} %param.16) | copy-start | bytes 196612
  6.5 4.7 %copy-start.3 = (bf16[128,256]{1,0:T(8,128)(2,1)S(1)}, bf16[128,256]{1,0:T(8,128)(2,1)}, u32[]{:S(2)}) copy-start(bf16[128,256]{1,0:T(8,128)(2,1)} %param.17) | copy-start | bytes 196612
  6.5 142.5 %all-gather.2.cloned.1.call-start = ((), (), s32[]{:S(2)}) async-start(), calls=%async_computation | async-start | bytes 17825792 | tf_op jit(solution)/shard_map/all_gather | solution.py:109
  7.3 192.4 %all-reduce.2.cloned.1.call-start = ((), (), s32[]{:S(2)}) async-start(), calls=%async_computation.1 | async-start | bytes 2097152 | tf_op jit(solution)/shard_map/psum | solution.py:118
  15.4 3.9 %collective-permute-start = (bf16[2,128,256]{1,2,0:T(8,128)(2,1)S(1)}, bf16[2,128,256]{1,2,0:T(8,128)(2,1)S(1)}, u32[]{:S(2)}, u32[]{:S(2)}) collective-permute-start(bf16[2,128,256]{1,2,0:T(8,128)(2,1)S(1)} %get-tuple-element.376), channel_id=1, source_target_pairs={{0,2},{2,4},{4,6},{6,8},{8,10},{10,12},{12,14},{14,16},{16,18},{18... | collective-permute-start | bytes 393224 | tf_op jit(solution)/shard_map/while/body/eval_jaxpr/ppermute | solution.py:14
  19.4 11.8 %collective-permute-start = (bf16[2,128,256]{1,2,0:T(8,128)(2,1)S(1)}, bf16[2,128,256]{1,2,0:T(8,128)(2,1)S(1)}, u32[]{:S(2)}, u32[]{:S(2)}) collective-permute-start(bf16[2,128,256]{1,2,0:T(8,128)(2,1)S(1)} %get-tuple-element.376), channel_id=1, source_target_pairs={{0,2},{2,4},{4,6},{6,8},{8,10},{10,12},{12,14},{14,16},{16,18},{18... | collective-permute-start | bytes 393224 | tf_op jit(solution)/shard_map/while/body/eval_jaxpr/ppermute | solution.py:14
  31.2 7.1 %collective-permute-start = (bf16[2,128,256]{1,2,0:T(8,128)(2,1)S(1)}, bf16[2,128,256]{1,2,0:T(8,128)(2,1)S(1)}, u32[]{:S(2)}, u32[]{:S(2)}) collective-permute-start(bf16[2,128,256]{1,2,0:T(8,128)(2,1)S(1)} %get-tuple-element.376), channel_id=1, source_target_pairs={{0,2},{2,4},{4,6},{6,8},{8,10},{10,12},{12,14},{14,16},{16,18},{18... | collective-permute-start | bytes 393224 | tf_op jit(solution)/shard_map/while/body/eval_jaxpr/ppermute | solution.py:14
  38.4 9.8 %collective-permute-start = (bf16[2,128,256]{1,2,0:T(8,128)(2,1)S(1)}, bf16[2,128,256]{1,2,0:T(8,128)(2,1)S(1)}, u32[]{:S(2)}, u32[]{:S(2)}) collective-permute-start(bf16[2,128,256]{1,2,0:T(8,128)(2,1)S(1)} %get-tuple-element.376), channel_id=1, source_target_pairs={{0,2},{2,4},{4,6},{6,8},{8,10},{10,12},{12,14},{14,16},{16,18},{18... | collective-permute-start | bytes 393224 | tf_op jit(solution)/shard_map/while/body/eval_jaxpr/ppermute | solution.py:14
  48.3 6.3 %collective-permute-start = (bf16[2,128,256]{1,2,0:T(8,128)(2,1)S(1)}, bf16[2,128,256]{1,2,0:T(8,128)(2,1)S(1)}, u32[]{:S(2)}, u32[]{:S(2)}) collective-permute-start(bf16[2,128,256]{1,2,0:T(8,128)(2,1)S(1)} %get-tuple-element.376), channel_id=1, source_target_pairs={{0,2},{2,4},{4,6},{6,8},{8,10},{10,12},{12,14},{14,16},{16,18},{18... | collective-permute-start | bytes 393224 | tf_op jit(solution)/shard_map/while/body/eval_jaxpr/ppermute | solution.py:14
  54.6 10.0 %collective-permute-start = (bf16[2,128,256]{1,2,0:T(8,128)(2,1)S(1)}, bf16[2,128,256]{1,2,0:T(8,128)(2,1)S(1)}, u32[]{:S(2)}, u32[]{:S(2)}) collective-permute-start(bf16[2,128,256]{1,2,0:T(8,128)(2,1)S(1)} %get-tuple-element.376), channel_id=1, source_target_pairs={{0,2},{2,4},{4,6},{6,8},{8,10},{10,12},{12,14},{14,16},{16,18},{18... | collective-permute-start | bytes 393224 | tf_op jit(solution)/shard_map/while/body/eval_jaxpr/ppermute | solution.py:14
  64.6 11.6 %collective-permute-start = (bf16[2,128,256]{1,2,0:T(8,128)(2,1)S(1)}, bf16[2,128,256]{1,2,0:T(8,128)(2,1)S(1)}, u32[]{:S(2)}, u32[]{:S(2)}) collective-permute-start(bf16[2,128,256]{1,2,0:T(8,128)(2,1)S(1)} %get-tuple-element.376), channel_id=1, source_target_pairs={{0,2},{2,4},{4,6},{6,8},{8,10},{10,12},{12,14},{14,16},{16,18},{18... | collective-permute-start | bytes 393224 | tf_op jit(solution)/shard_map/while/body/eval_jaxpr/ppermute | solution.py:14
  76.3 13.7 %collective-permute-start = (bf16[2,128,256]{1,2,0:T(8,128)(2,1)S(1)}, bf16[2,128,256]{1,2,0:T(8,128)(2,1)S(1)}, u32[]{:S(2)}, u32[]{:S(2)}) collective-permute-start(bf16[2,128,256]{1,2,0:T(8,128)(2,1)S(1)} %get-tuple-element.376), channel_id=1, source_target_pairs={{0,2},{2,4},{4,6},{6,8},{8,10},{10,12},{12,14},{14,16},{16,18},{18... | collective-permute-start | bytes 393224 | tf_op jit(solution)/shard_map/while/body/eval_jaxpr/ppermute | solution.py:14
  149.0 8.2 %copy-start.1 = (bf16[128,2048]{1,0:T(8,128)(2,1)S(1)}, bf16[128,2048]{1,0:T(8,128)(2,1)}, u32[]{:S(2)}) copy-start(bf16[128,2048]{1,0:T(8,128)(2,1)} %param.18) | copy-start | bytes 1572868
  158.6 44.1 %copy-start.4 = (f32[2048]{0:T(1024)S(1)}, f32[2048]{0:T(1024)}, u32[]{:S(2)}) copy-start(f32[2048]{0:T(1024)} %param.20) | copy-start | bytes 24580
Sparse Core Ops, SparseCore 0:
  9.5 139.4 all-gather.1
  158.7 40.9 all-reduce.1
where the time goes:
time: 212 us; the launch traced here: 211 us
  waiting for transfers between devices  100 us (47%)
  starting transfers between devices  62.1 us (29%)
  other arithmetic  15.7 us (7%)
  between operations  14.2 us (7%)
  matrix products  11.3 us (5%)
  loops' own time  5.64 us (3%)
    ppermute x8, starting transfers between devices, shifted(): return lax.ppermute(block, axis, route)  62 us
    all_gather x1, waiting for transfers between devices, on_device(): lax.all_gather(out_weight, ('section', 'srv'), axis=1, tiled=True)  58.3 us
    psum x1, waiting for transfers between devices, on_device(): whole = lax.psum(placed.astype(jnp.bfloat16), 'tp').astype(jnp.float32)  41.1 us
    dot_general x1, matrix products, on_device(): jnp.dot(attended, lax.all_gather(out_weight, ('section', 'srv'), axis=1,...  8.18 us
    and x9, other arithmetic, absorb(): (key_pos[None, :] >= row_first[:, None]) & (key_pos[None, :] < row_limit[...  7.8 us
    another operation x1, loops' own time, on_device(): lax.fori_loop(1, span, turn_step, (carry, jnp.stack([keys, values], axis=...  5.48 us
  transfers between devices with their start and end apart: 10, of which 2 were waited for; matrix products, arithmetic and copies ran while one was open for 7% of the time, Pallas kernels for 0%

commit v1 on v0

--- a/solution.py
+++ b/solution.py
@@ -115,7 +115,8 @@
         jnp.float32
     )
     placed = lax.dynamic_update_slice_in_dim(partial_sum, own_part, offset, 1)
-    whole = lax.psum(placed.astype(jnp.bfloat16), "tp").astype(jnp.float32)
+    play_slot = lambda u: jnp.sum(lax.all_gather(u, "tp"), axis=0)
+    whole = play_slot(placed.astype(jnp.bfloat16)).astype(jnp.float32)
     hidden = lax.dynamic_slice_in_dim(whole, offset, width, 1)
     squares = jnp.sum(whole * whole, axis=1)
     inverse = lax.rsqrt(squares / D + 1e-06)

time: 212 us -> 206 us (0.972)
  waiting for transfers between devices: 100 us -> 93.7 us
    psum x1 -> x0, waiting for transfers between devices: 41.1 us -> none  [on_device(): whole = lax.psum(placed.astype(jnp.bfloat16), 'tp').astype(jnp.float32)]
    all_gather x0 -> x1, waiting for transfers between devices: none -> 34 us  [on_device(): play_slot = lambda u: jnp.sum(lax.all_gather(u, 'tp'), axis=0)]
where the time goes in v1:
time: 206 us; the launch traced here: 204 us
  waiting for transfers between devices  93.7 us (45%)
  starting transfers between devices  62.1 us (30%)
  other arithmetic  15.3 us (7%)
  between operations  14.2 us (7%)
  matrix products  11.3 us (5%)
  loops' own time  5.64 us (3%)
  local copies, waits for them, and re-layouts  2.1 us (1%)
    ppermute x8, starting transfers between devices, shifted(): return lax.ppermute(block, axis, route)  62 us
    all_gather x1, waiting for transfers between devices, on_device(): lax.all_gather(out_weight, ('section', 'srv'), axis=1, tiled=True)  59 us
    all_gather x1, waiting for transfers between devices, on_device(): play_slot = lambda u: jnp.sum(lax.all_gather(u, 'tp'), axis=0)  34 us
    dot_general x1, matrix products, on_device(): jnp.dot(attended, lax.all_gather(out_weight, ('section', 'srv'), axis=1,...  8.18 us
    and x9, other arithmetic, absorb(): (key_pos[None, :] >= row_first[:, None]) & (key_pos[None, :] < row_limit[...  7.8 us
    another operation x1, loops' own time, on_device(): lax.fori_loop(1, span, turn_step, (carry, jnp.stack([keys, values], axis=...  5.48 us
  transfers between devices with their start and end apart: 10, of which 2 were waited for; matrix products, arithmetic and copies ran while one was open for 7% of the time, Pallas kernels for 0%

profile of v1, /device:TPU:0, one launch (start us, length us, event | category | flops | bytes accessed | tf_op | source)
XLA Modules:
  0.0 204.2 jit_solution(7835478841868971317)
XLA Ops:
  8.2 1.1 copy.50
  11.4 3.9 %conditional.2 = (f32[2,1024]{1,0:T(2,128)}, f32[2,1024]{1,0:T(2,128)S(1)}, f32[2,1024,128]{2,1,0:T(8,128)S(1)}) conditional(s32[]{:T(128)} %convert_element_type.43, () %tuple.34, (pred[1024,128]{0,1:T(8,128)(4,1)S(1)}, bf16[128,256]{1,0:T(8,128)(2,1)S(1)}, bf16[2,1024,128]{2,1,0:T(8,128)(2,1)S(1)}, bf16[128,256]{1,0:T(8,128)(2,1)S(1)}) %tuple.84), branch_computations={%region_3.4_spmd, %region_4.7_spmd} | conditional | flops 136847360 | bytes 5333016 | solution.py:67
  12.4 1.3 convolution_add_fusion
  13.7 0.9 fusion.6
  15.3 74.7 %while.20 = (s32[]{:T(128)}, f32[2,1024]{1,0:T(2,128)}, f32[2,1024]{1,0:T(2,128)S(1)}, f32[2,1024,128]{2,1,0:T(8,128)S(1)}, bf16[2,128,256]{1,2,0:T(8,128)(2,1)S...) while((s32[]{:T(128)}, f32[2,1024]{1,0:T(2,128)}, ...), condition=%wide.region_13.14_spmd.clone, body=%wide.region_7.13_spmd.clone.sunk | while | flops 137629824 | bytes 7620895 | solution.py:105
  15.4 2.4 %collective-permute-start = (bf16[2,128,256]{1,2,0:T(8,128)(2,1)S(1)}, bf16[2,128,256]{1,2,0:T(8,128)(2,1)S(1)}, u32[]{:S(2)}, u32[]{:S(2)}) collective-permute-start(bf16[2,128,256]{1,2,0:T(8,128)(2,1)S(1)} %get-tuple-element.376), channel_id=1, source_target_pairs={{0,2},{2,4},{4,6},{6,8},{8,10},{10,12},{12,14},{14,16},{16,18},{18... | collective-permute-start | bytes 393224 | tf_op jit(solution)/shard_map/while/body/eval_jaxpr/ppermute | solution.py:14
  17.8 0.9 compare_and_fusion.4
  19.4 10.3 %collective-permute-start = (bf16[2,128,256]{1,2,0:T(8,128)(2,1)S(1)}, bf16[2,128,256]{1,2,0:T(8,128)(2,1)S(1)}, u32[]{:S(2)}, u32[]{:S(2)}) collective-permute-start(bf16[2,128,256]{1,2,0:T(8,128)(2,1)S(1)} %get-tuple-element.376), channel_id=1, source_target_pairs={{0,2},{2,4},{4,6},{6,8},{8,10},{10,12},{12,14},{14,16},{16,18},{18... | collective-permute-start | bytes 393224 | tf_op jit(solution)/shard_map/while/body/eval_jaxpr/ppermute | solution.py:14
  29.6 0.9 compare_and_fusion.4
  31.2 5.6 %collective-permute-start = (bf16[2,128,256]{1,2,0:T(8,128)(2,1)S(1)}, bf16[2,128,256]{1,2,0:T(8,128)(2,1)S(1)}, u32[]{:S(2)}, u32[]{:S(2)}) collective-permute-start(bf16[2,128,256]{1,2,0:T(8,128)(2,1)S(1)} %get-tuple-element.376), channel_id=1, source_target_pairs={{0,2},{2,4},{4,6},{6,8},{8,10},{10,12},{12,14},{14,16},{16,18},{18... | collective-permute-start | bytes 393224 | tf_op jit(solution)/shard_map/while/body/eval_jaxpr/ppermute | solution.py:14
  36.9 0.9 compare_and_fusion.4
  38.4 8.3 %collective-permute-start = (bf16[2,128,256]{1,2,0:T(8,128)(2,1)S(1)}, bf16[2,128,256]{1,2,0:T(8,128)(2,1)S(1)}, u32[]{:S(2)}, u32[]{:S(2)}) collective-permute-start(bf16[2,128,256]{1,2,0:T(8,128)(2,1)S(1)} %get-tuple-element.376), channel_id=1, source_target_pairs={{0,2},{2,4},{4,6},{6,8},{8,10},{10,12},{12,14},{14,16},{16,18},{18... | collective-permute-start | bytes 393224 | tf_op jit(solution)/shard_map/while/body/eval_jaxpr/ppermute | solution.py:14
  46.7 0.9 compare_and_fusion.4
  48.3 4.7 %collective-permute-start = (bf16[2,128,256]{1,2,0:T(8,128)(2,1)S(1)}, bf16[2,128,256]{1,2,0:T(8,128)(2,1)S(1)}, u32[]{:S(2)}, u32[]{:S(2)}) collective-permute-start(bf16[2,128,256]{1,2,0:T(8,128)(2,1)S(1)} %get-tuple-element.376), channel_id=1, source_target_pairs={{0,2},{2,4},{4,6},{6,8},{8,10},{10,12},{12,14},{14,16},{16,18},{18... | collective-permute-start | bytes 393224 | tf_op jit(solution)/shard_map/while/body/eval_jaxpr/ppermute | solution.py:14
  53.0 0.9 compare_and_fusion.4
  54.6 8.4 %collective-permute-start = (bf16[2,128,256]{1,2,0:T(8,128)(2,1)S(1)}, bf16[2,128,256]{1,2,0:T(8,128)(2,1)S(1)}, u32[]{:S(2)}, u32[]{:S(2)}) collective-permute-start(bf16[2,128,256]{1,2,0:T(8,128)(2,1)S(1)} %get-tuple-element.376), channel_id=1, source_target_pairs={{0,2},{2,4},{4,6},{6,8},{8,10},{10,12},{12,14},{14,16},{16,18},{18... | collective-permute-start | bytes 393224 | tf_op jit(solution)/shard_map/while/body/eval_jaxpr/ppermute | solution.py:14
  64.6 10.0 %collective-permute-start = (bf16[2,128,256]{1,2,0:T(8,128)(2,1)S(1)}, bf16[2,128,256]{1,2,0:T(8,128)(2,1)S(1)}, u32[]{:S(2)}, u32[]{:S(2)}) collective-permute-start(bf16[2,128,256]{1,2,0:T(8,128)(2,1)S(1)} %get-tuple-element.376), channel_id=1, source_target_pairs={{0,2},{2,4},{4,6},{6,8},{8,10},{10,12},{12,14},{14,16},{16,18},{18... | collective-permute-start | bytes 393224 | tf_op jit(solution)/shard_map/while/body/eval_jaxpr/ppermute | solution.py:14
  76.2 12.2 %collective-permute-start = (bf16[2,128,256]{1,2,0:T(8,128)(2,1)S(1)}, bf16[2,128,256]{1,2,0:T(8,128)(2,1)S(1)}, u32[]{:S(2)}, u32[]{:S(2)}) collective-permute-start(bf16[2,128,256]{1,2,0:T(8,128)(2,1)S(1)} %get-tuple-element.376), channel_id=1, source_target_pairs={{0,2},{2,4},{4,6},{6,8},{8,10},{10,12},{12,14},{14,16},{16,18},{18... | collective-permute-start | bytes 393224 | tf_op jit(solution)/shard_map/while/body/eval_jaxpr/ppermute | solution.py:14
  90.7 59.0 %all-gather.4.cloned.1.call-done = bf16[2048,4096]{1,0:T(8,128)(2,1)} async-done(((bf16[2048,256]{1,0:T(8,128)(2,1)}), bf16[2048,4096]{1,0:T(8,128)(2,1)}) %all-gather.4.cloned.1.call-update) | async-done | bytes 16777232 | tf_op jit(solution)/shard_map/all_gather | solution.py:109
  149.7 8.2 %fusion.34 = f32[128,4096]{1,0:T(8,128)S(1)} fusion(bf16[128,2048]{0,1:T(8,128)(2,1)S(1)} %bitcast.62, bf16[2048,4096]{1,0:T(8,128)(2,1)} %all-gather.4.cloned.1.call-done), kind=kOutput, calls=%fused_computation.65 | convolution fusion | flops 2147483648 | bytes 19398656 | tf_op jit(solution)/shard_map/dot_general | solution.py:107
  158.0 1.1 convert_element_type.49
  159.2 34.0 %all-gather.6.cloned.1.call-done = bf16[256,4096]{1,0:T(8,128)(2,1)} async-done(((bf16[128,4096]{1,0:T(8,128)(2,1)}), bf16[256,4096]{1,0:T(8,128)(2,1)}) %all-gather.6.cloned.1.call-update) | async-done | bytes 2097168 | tf_op jit(solution)/shard_map/all_gather | solution.py:118
  193.2 2.1 %reduce_sum.58 = bf16[128,4096]{1,0:T(8,128)(2,1)S(1)} reduce(bf16[2,128,4096]{2,1,0:T(8,128)(2,1)} %bitcast.64, bf16[]{:T(256)} %constant.93.clone.1), dimensions={0}, to_apply=%region_14.15 | reduce | flops 524288 | bytes 3145730 | tf_op jit(solution)/shard_map/reduce_sum | solution.py:118
  196.0 1.4 fusion.27
  (82 shorter events, 9.0 us)
Async XLA Ops:
  6.5 189.3 %copy-start = (f32[8,2048]{1,0:T(8,128)S(1)}, f32[8,2048]{1,0:T(8,128)}, u32[]{:S(2)}) copy-start(f32[8,2048]{1,0:T(8,128)} %param.21) | copy-start | bytes 196612
  6.5 3.0 %copy-start.6 = (s32[1,4]{1,0:T(1,128)S(1)}, s32[1,4]{1,0:T(1,128)}, u32[]{:S(2)}) copy-start(s32[1,4]{1,0:T(1,128)} %param.22) | copy-start | bytes 52
  6.5 3.0 %copy-start.5 = (s32[1,4]{1,0:T(1,128)S(1)}, s32[1,4]{1,0:T(1,128)}, u32[]{:S(2)}) copy-start(s32[1,4]{1,0:T(1,128)} %param.23) | copy-start | bytes 52
  6.5 4.6 %copy-start.2 = (bf16[128,256]{1,0:T(8,128)(2,1)S(1)}, bf16[128,256]{1,0:T(8,128)(2,1)}, u32[]{:S(2)}) copy-start(bf16[128,256]{1,0:T(8,128)(2,1)} %param.16) | copy-start | bytes 196612
  6.5 4.7 %copy-start.3 = (bf16[128,256]{1,0:T(8,128)(2,1)S(1)}, bf16[128,256]{1,0:T(8,128)(2,1)}, u32[]{:S(2)}) copy-start(bf16[128,256]{1,0:T(8,128)(2,1)} %param.17) | copy-start | bytes 196612
  6.5 143.1 %all-gather.4.cloned.1.call-start = ((), (), s32[]{:S(2)}) async-start(), calls=%async_computation | async-start | bytes 17825792 | tf_op jit(solution)/shard_map/all_gather | solution.py:109
  7.3 185.9 %all-gather.6.cloned.1.call-start = ((), (), s32[]{:S(2)}) async-start(), calls=%async_computation.1 | async-start | bytes 3145728 | tf_op jit(solution)/shard_map/all_gather | solution.py:118
  15.4 3.9 %collective-permute-start = (bf16[2,128,256]{1,2,0:T(8,128)(2,1)S(1)}, bf16[2,128,256]{1,2,0:T(8,128)(2,1)S(1)}, u32[]{:S(2)}, u32[]{:S(2)}) collective-permute-start(bf16[2,128,256]{1,2,0:T(8,128)(2,1)S(1)} %get-tuple-element.376), channel_id=1, source_target_pairs={{0,2},{2,4},{4,6},{6,8},{8,10},{10,12},{12,14},{14,16},{16,18},{18... | collective-permute-start | bytes 393224 | tf_op jit(solution)/shard_map/while/body/eval_jaxpr/ppermute | solution.py:14
  19.4 11.8 %collective-permute-start = (bf16[2,128,256]{1,2,0:T(8,128)(2,1)S(1)}, bf16[2,128,256]{1,2,0:T(8,128)(2,1)S(1)}, u32[]{:S(2)}, u32[]{:S(2)}) collective-permute-start(bf16[2,128,256]{1,2,0:T(8,128)(2,1)S(1)} %get-tuple-element.376), channel_id=1, source_target_pairs={{0,2},{2,4},{4,6},{6,8},{8,10},{10,12},{12,14},{14,16},{16,18},{18... | collective-permute-start | bytes 393224 | tf_op jit(solution)/shard_map/while/body/eval_jaxpr/ppermute | solution.py:14
  31.2 7.1 %collective-permute-start = (bf16[2,128,256]{1,2,0:T(8,128)(2,1)S(1)}, bf16[2,128,256]{1,2,0:T(8,128)(2,1)S(1)}, u32[]{:S(2)}, u32[]{:S(2)}) collective-permute-start(bf16[2,128,256]{1,2,0:T(8,128)(2,1)S(1)} %get-tuple-element.376), channel_id=1, source_target_pairs={{0,2},{2,4},{4,6},{6,8},{8,10},{10,12},{12,14},{14,16},{16,18},{18... | collective-permute-start | bytes 393224 | tf_op jit(solution)/shard_map/while/body/eval_jaxpr/ppermute | solution.py:14
  38.4 9.8 %collective-permute-start = (bf16[2,128,256]{1,2,0:T(8,128)(2,1)S(1)}, bf16[2,128,256]{1,2,0:T(8,128)(2,1)S(1)}, u32[]{:S(2)}, u32[]{:S(2)}) collective-permute-start(bf16[2,128,256]{1,2,0:T(8,128)(2,1)S(1)} %get-tuple-element.376), channel_id=1, source_target_pairs={{0,2},{2,4},{4,6},{6,8},{8,10},{10,12},{12,14},{14,16},{16,18},{18... | collective-permute-start | bytes 393224 | tf_op jit(solution)/shard_map/while/body/eval_jaxpr/ppermute | solution.py:14
  48.3 6.3 %collective-permute-start = (bf16[2,128,256]{1,2,0:T(8,128)(2,1)S(1)}, bf16[2,128,256]{1,2,0:T(8,128)(2,1)S(1)}, u32[]{:S(2)}, u32[]{:S(2)}) collective-permute-start(bf16[2,128,256]{1,2,0:T(8,128)(2,1)S(1)} %get-tuple-element.376), channel_id=1, source_target_pairs={{0,2},{2,4},{4,6},{6,8},{8,10},{10,12},{12,14},{14,16},{16,18},{18... | collective-permute-start | bytes 393224 | tf_op jit(solution)/shard_map/while/body/eval_jaxpr/ppermute | solution.py:14
  54.6 10.0 %collective-permute-start = (bf16[2,128,256]{1,2,0:T(8,128)(2,1)S(1)}, bf16[2,128,256]{1,2,0:T(8,128)(2,1)S(1)}, u32[]{:S(2)}, u32[]{:S(2)}) collective-permute-start(bf16[2,128,256]{1,2,0:T(8,128)(2,1)S(1)} %get-tuple-element.376), channel_id=1, source_target_pairs={{0,2},{2,4},{4,6},{6,8},{8,10},{10,12},{12,14},{14,16},{16,18},{18... | collective-permute-start | bytes 393224 | tf_op jit(solution)/shard_map/while/body/eval_jaxpr/ppermute | solution.py:14
  64.6 11.5 %collective-permute-start = (bf16[2,128,256]{1,2,0:T(8,128)(2,1)S(1)}, bf16[2,128,256]{1,2,0:T(8,128)(2,1)S(1)}, u32[]{:S(2)}, u32[]{:S(2)}) collective-permute-start(bf16[2,128,256]{1,2,0:T(8,128)(2,1)S(1)} %get-tuple-element.376), channel_id=1, source_target_pairs={{0,2},{2,4},{4,6},{6,8},{8,10},{10,12},{12,14},{14,16},{16,18},{18... | collective-permute-start | bytes 393224 | tf_op jit(solution)/shard_map/while/body/eval_jaxpr/ppermute | solution.py:14
  76.2 13.8 %collective-permute-start = (bf16[2,128,256]{1,2,0:T(8,128)(2,1)S(1)}, bf16[2,128,256]{1,2,0:T(8,128)(2,1)S(1)}, u32[]{:S(2)}, u32[]{:S(2)}) collective-permute-start(bf16[2,128,256]{1,2,0:T(8,128)(2,1)S(1)} %get-tuple-element.376), channel_id=1, source_target_pairs={{0,2},{2,4},{4,6},{6,8},{8,10},{10,12},{12,14},{14,16},{16,18},{18... | collective-permute-start | bytes 393224 | tf_op jit(solution)/shard_map/while/body/eval_jaxpr/ppermute | solution.py:14
  149.7 8.2 %copy-start.1 = (bf16[128,2048]{1,0:T(8,128)(2,1)S(1)}, bf16[128,2048]{1,0:T(8,128)(2,1)}, u32[]{:S(2)}) copy-start(bf16[128,2048]{1,0:T(8,128)(2,1)} %param.18) | copy-start | bytes 1572868
  195.3 0.7 copy-start.4
Sparse Core Ops, SparseCore 0:
  9.5 140.1 all-gather.3
  159.3 33.8 all-gather.5
